TPU v7x, 256 devices: a 8x8x2 block of a 8x8x16 slice. The times are simulated.
256 devices in a mesh: member: 2 (over z), lat: 128 (over x, y, core).
Axes of the slice: x: 8, y: 8, z: 2, core: 2. Of those that a mesh axis runs over, the one named last changes fastest.
The devices are a block of a 8x8x16 slice.
Arguments:
- height: float32 [1024, 32, 1440], P(('member', 'lat')), parts along dimension 0, may hold values from -6 to 6
- zonal_courant: float32 [1024, 32, 1440], P(('member', 'lat')), parts along dimension 0, may hold values from -1.5 to 1.5
- merid_courant: float32 [1024, 32, 1440], P(('member', 'lat')), parts along dimension 0, may hold values from -1.5 to 1.5
- rates: float32 [64], P('member'), parts along dimension 0, may hold values from 0.05 to 0.5
- thresholds: float32 [64], P('member'), parts along dimension 0, may hold values from -3 to 3
- flags: int32 [512], replicated, may hold values from 0 to 1, as said below
- cutoffs: int32 [512], replicated, may hold values from 45 to 360
Outputs:
- filtered_height: float32 [1024, 32, 1440], P(('member', 'lat')), parts along dimension 0
There are 2 independent parts, one for each index of `member`. A program takes and returns all parts, laid end to end along the dimension named above; an argument that names none is the same for every part. Nothing has to cross between parts.
Inputs may be any that keep to these rules, and one draw needn't show every extreme that they name: flags is 1 on a southern band of rows that starts at row 0 and on a northern band that ends at row 511, each band 512 // 8 to 128 rows long, and 0 on all other rows.
All inputs are finite; a program needn't handle non-finite values.
Results may differ from a plain program's by a relative error of at most 0.00007.
Values sent between devices are 32-bit elements; how exact they have to be, the bound alone decides.
A program may use at most 64 MiB of HBM per device.

v0:
```python
import jax
import jax.numpy as jnp
from jax import lax
from jax.sharding import Mesh
from jax.sharding import PartitionSpec as P

LAT = ("lat_0", "lat_1", "lat_2")
MEMBER_LAT = ("member", "lat_0", "lat_1", "lat_2")


def padded_2(cells, sides, width):
    for axis, dim in sides:
        count = lax.axis_size(axis)
        ends = count - 1
        head = lax.slice_in_dim(cells, 0, width, axis=dim)
        tail = lax.slice_in_dim(cells, cells.shape[dim] - width, cells.shape[dim], axis=dim)
        cells = jnp.concatenate(
            [
                lax.ppermute(tail, axis, [(i, (i + 1) % count) for i in range(ends)]),
                cells,
                lax.ppermute(head, axis, [((i + 1) % count, i) for i in range(ends)]),
            ],
            axis=dim,
        )
    return cells


def one_axis_at_a_time(array, axes):
    for axis in axes:
        array = lax.psum(array, axis)
    return array


def transform_table(nlon, nkp):
    points = jnp.arange(nlon, dtype=jnp.int32)
    waves = jnp.arange(nkp, dtype=jnp.int32)
    phase = points[:, None] * waves[None, :] % nlon
    angle = 2.0 * jnp.pi / nlon * phase.astype(jnp.float32)
    return jnp.concatenate([jnp.cos(angle), jnp.sin(angle)], axis=1)


def wave_weights(nlon, nkp):
    waves = jnp.arange(nkp, dtype=jnp.int32)
    interior = jnp.where((waves > 0) & (waves < nlon // 2), 2.0, 1.0)
    return jnp.where(waves <= nlon // 2, interior, 0.0).astype(jnp.float32) / nlon


def damping(row_flags, row_cutoffs, nkp):
    waves = jnp.maximum(jnp.arange(nkp), 1).astype(jnp.float32)
    ratio = row_cutoffs.astype(jnp.float32)[:, None] / waves[None, :]
    factor = jnp.minimum(1.0, ratio * ratio)
    return jnp.where(row_flags[:, None] > 0, factor, 1.0)


def filter_units(flat, damp, table, weights):
    highest = lax.Precision.HIGHEST
    spectrum = jnp.dot(flat, table, precision=highest, preferred_element_type=jnp.float32)
    factor = (1.0 - damp) * weights[None, :]
    scaled = spectrum * jnp.concatenate([factor, factor], axis=1)
    dims = (((1,), (1,)), ((), ()))
    removed = lax.dot_general(
        scaled, table, dims, precision=highest, preferred_element_type=jnp.float32
    )
    return flat - removed


def filtered_or_kept(block, row_flags, row_cutoffs, table, weights):
    rows, levels, nlon = block.shape
    damp = damping(row_flags, row_cutoffs, weights.shape[0])
    unit_damp = jnp.broadcast_to(damp[:, None, :], (rows, levels, damp.shape[1])).reshape(
        rows * levels, damp.shape[1]
    )

    def apply_filter(data):
        return filter_units(data.reshape(rows * levels, nlon), unit_damp, table, weights).reshape(
            rows, levels, nlon
        )

    def keep_block(data):
        return data

    return lax.cond(jnp.any(row_flags > 0), apply_filter, keep_block, block)


def face_fluxes(rows_height, rows_speed, face_cos, count):
    face_value = (
        7.0 * (rows_height[1 : count + 1] + rows_height[2 : count + 2])
        - (rows_height[0:count] + rows_height[3 : count + 3])
    ) / 12.0
    speed = 0.5 * (rows_speed[0:count] + rows_speed[1 : count + 1]) * face_cos[:, None, None]
    return speed * face_value


def face_cosines(face_ids, nlat):
    return jnp.where(
        (face_ids > 0) & (face_ids < nlat),
        jnp.sin(jnp.pi * face_ids.astype(jnp.float32) / nlat),
        jnp.float32(0.0),
    )


def local(height, zonal_courant, merid_courant, rates, thresholds, flags, cutoffs):
    lat_rows, levels, nlon = height.shape
    devices = lax.axis_size(LAT)
    position = lax.axis_index(LAT)
    first_row = position * lat_rows
    nlat = lat_rows * devices
    local_rows = first_row + jnp.arange(lat_rows, dtype=jnp.int32)
    cos_rows = jnp.sin(jnp.pi * (local_rows.astype(jnp.float32) + 0.5) / nlat)
    faces = first_row + jnp.arange(lat_rows + 1, dtype=jnp.int32)
    cos_faces = face_cosines(faces, nlat)
    padded = padded_2(jnp.stack([height, merid_courant]), ((LAT, 1),), 2)
    east = jnp.roll(height, -1, axis=2)
    west = jnp.roll(height, 1, axis=2)
    far_east = jnp.roll(height, -2, axis=2)
    face_height = (7.0 * (height + east) - (west + far_east)) / 12.0
    face_speed = 0.5 * (zonal_courant + jnp.roll(zonal_courant, -1, axis=2))
    zonal_flux = face_speed * face_height
    zonal_div = zonal_flux - jnp.roll(zonal_flux, 1, axis=2)
    source = -rates[None, :, None] * jax.nn.softplus(height - thresholds[None, :, None])
    partial_sums = jnp.sum(jnp.sum(source, axis=2) * cos_rows[:, None], axis=0)
    totals = one_axis_at_a_time(partial_sums, LAT)
    all_rows = jnp.arange(nlat, dtype=jnp.int32)
    area = nlon * jnp.sum(jnp.sin(jnp.pi * (all_rows.astype(jnp.float32) + 0.5) / nlat))
    level_mean = totals / area
    padded_height = padded[0]
    padded_speed = padded[1]
    count = lat_rows + 1
    merid_flux = face_fluxes(padded_height, padded_speed[1:], cos_faces, count)
    merid_div = (merid_flux[1:] - merid_flux[:-1]) / cos_rows[:, None, None]
    updated = height - zonal_div - merid_div + source - level_mean[None, :, None]
    nkp = (nlon // 2 + 128) // 128 * 128
    table = transform_table(nlon, nkp)
    weights = wave_weights(nlon, nkp)
    row_flags = lax.dynamic_slice_in_dim(flags, first_row, lat_rows)
    row_cutoffs = lax.dynamic_slice_in_dim(cutoffs, first_row, lat_rows)
    result = filtered_or_kept(updated, row_flags, row_cutoffs, table, weights)
    return result


def solution(mesh):
    finer = Mesh(
        mesh.devices.reshape(mesh.shape["member"], 8, 8, 2), ("member", "lat_0", "lat_1", "lat_2")
    )
    placed = (
        P(MEMBER_LAT, None, None),
        P(MEMBER_LAT, None, None),
        P(MEMBER_LAT, None, None),
        P("member"),
        P("member"),
        P(),
        P(),
    )
    return jax.shard_map(
        local, mesh=finer, in_specs=placed, out_specs=P(MEMBER_LAT, None, None), check_vma=False
    )
```

profile of v0, /device:TPU:513, one launch (start us, length us, event | category | flops | bytes accessed | tf_op | source)
XLA Modules:
  0.0 114.5 jit_solution(6825483343422072671)
XLA Ops:
  0.0 0.0 copy-start
  0.0 0.0 copy-start.2
  0.0 2.5 %fusion.17 = (f32[2,2,32,1440]{3,2,1,0:T(8,128)}, f32[2,2,32,1440]{3,2,1,0:T(8,128)S(1)}) fusion(f32[1,4,32,1440]{3,2,1,0:T(8,128)} %bitcast.21, f32[1,4,32,1440]{3,2,1,0:T(8,128)} %bitcast.27), kind=kLoop, calls=%fused_computation.33 | loop fusion | flops 368640 | bytes 2949120 | tf_op jit(solution)/shard_map/stack | solution.py:112
  2.5 5.7 %collective-permute-start = (f32[2,2,32,1440]{3,2,1,0:T(8,128)}, f32[2,2,32,1440]{3,2,1,0:T(8,128)}, u32[]{:S(2)}, u32[]{:S(2)}) collective-permute-start(f32[2,2,32,1440]{3,2,1,0:T(8,128)} %get-tuple-element.115), channel_id=1, source_target_pairs={{0,1},{1,2},{2,3},{3,4},{4,5},{5,6},{6,7},{7,8},{8,9},{9,10},{10,1... | collective-permute-start | bytes 2211848 | tf_op jit(solution)/shard_map/ppermute | solution.py:19
  8.2 18.8 %collective-permute-start.1 = (f32[2,2,32,1440]{3,2,1,0:T(8,128)S(1)}, f32[2,2,32,1440]{3,2,1,0:T(8,128)}, u32[]{:S(2)}, u32[]{:S(2)}) collective-permute-start(f32[2,2,32,1440]{3,2,1,0:T(8,128)S(1)} %get-tuple-element.116), channel_id=1, source_target_pairs={{1,0},{2,1},{3,2},{4,3},{5,4},{6,5},{7,6},{8,7},{9,8},{10,9},{11,1... | collective-permute-start | bytes 2211848 | tf_op jit(solution)/shard_map/ppermute | solution.py:21
  27.1 1.6 %fusion.33 = (f32[4,32,1439]{2,1,0:T(8,128)S(1)}, f32[4,32,1439]{2,1,0:T(8,128)S(1)}) fusion(f32[4,32,1440]{2,1,0:T(8,128)} %param.9), kind=kLoop, calls=%fused_computation.63 | loop fusion | bytes 2947072 | tf_op jit(solution)/shard_map/jit(_roll_static)/slice | solution.py:114
  28.8 0.0 copy-done
  28.8 0.1 fusion.32
  28.9 0.3 slice.95
  29.2 0.0 copy-done.2
  29.2 0.3 slice.89
  29.5 0.7 sine_reduce_fusion
  30.2 0.0 copy-start.5
  30.2 0.0 slice-start
  30.2 0.0 copy-start.4
  30.2 19.5 %fusion.7 = (f32[1440,768]{1,0:T(8,128)}, f32[1440,768]{1,0:T(8,128)}) fusion(), kind=kLoop, calls=%fused_computation.15 | loop fusion | flops 9953280 | bytes 8847360 | tf_op jit(solution)/shard_map/sin | solution.py:39
  49.7 0.0 copy-done.5
  49.7 0.0 slice-done
  49.8 0.0 copy-done.4
  49.8 0.9 fusion.29
  50.7 0.1 multiply_reduce_fusion
  50.8 10.7 %psum.21 = f32[32]{0:T(128)S(1)} all-reduce(f32[32]{0:T(128)S(1)} %multiply_reduce_fusion), channel_id=1, replica_groups=mesh['member'=2,'lat_0'=8,'lat_1'=8,'lat_2'=2] {'lat_0'}, use_global_device_ids=true, to_apply=%region_3.4 | all-reduce | flops 32 | bytes 256 | tf_op jit(solution)/shard_map/psum | solution.py:30
  61.5 10.7 %psum.22 = f32[32]{0:T(128)S(1)} all-reduce(f32[32]{0:T(128)S(1)} %psum.21), channel_id=1, replica_groups=mesh['member'=2,'lat_0'=8,'lat_1'=8,'lat_2'=2] {'lat_1'}, use_global_device_ids=true, to_apply=%region_4.5 | all-reduce | flops 32 | bytes 256 | tf_op jit(solution)/shard_map/psum | solution.py:30
  72.3 8.5 %psum.23 = f32[32]{0:T(128)S(1)} all-reduce(f32[32]{0:T(128)S(1)} %psum.22), channel_id=1, replica_groups=mesh['member'=2,'lat_0'=8,'lat_1'=8,'lat_2'=2] {'lat_2'}, use_global_device_ids=true, to_apply=%region_5.6 | all-reduce | flops 32 | bytes 256 | tf_op jit(solution)/shard_map/psum | solution.py:30
  80.7 0.1 slice.109
  80.8 1.4 %fusion.31 = (pred[]{:T(512)}, pred[4]{0:T(512)(128)(4,1)S(1)}) fusion(s32[512]{0:T(512)} %param.14, s32[]{:T(128)S(6)} %select_n.50), kind=kLoop, calls=%fused_computation.61 | loop fusion | flops 7 | bytes 25 | tf_op jit(solution)/shard_map/reduce_or | solution.py:82
  82.2 0.8 dynamic-slice_convert_fusion
  84.2 0.0 copy-start.3
  84.3 8.2 %pad_maximum_fusion = f32[1440,1536]{1,0:T(8,128)} fusion(f32[1440,768]{1,0:T(8,128)} %get-tuple-element.123, f32[1440,768]{1,0:T(8,128)} %get-tuple-element.124), kind=kLoop, calls=%fused_computation.8 | loop fusion | flops 2211840 | bytes 17694720 | tf_op jit(solution)/shard_map/concatenate | solution.py:39
  92.4 0.0 collective-permute-done
  92.4 0.0 collective-permute-done.1
  92.4 0.0 copy-done.3
  92.4 1.9 %maximum_maximum_fusion = (f32[2,6,32,1440]{3,2,1,0:T(8,128)S(1)}, f32[2,6,32,1440]{3,2,1,0:T(8,128)S(1)}) fusion(f32[1,4,32,1440]{3,2,1,0:T(8,128)S(1)} %bitcast.28, f32[1,4,32,1440]{3,2,1,0:T(8,128)S(1)} %bitcast.22, f32[2,2,32,1440]{3,2,1,0:T(8,128)} %collective-permute-done, f32[2,2,32,1440]{3,2,1,0:T(8,128)} %collective-permute-done.1), kind=kLoop, calls=%fused_computation.18 | loop fusion | flops 2211840 | bytes 7372800 | tf_op jit(solution)/shard_map/concatenate | solution.py:17
  94.4 0.5 fusion.13
  94.9 0.7 fusion.22
  95.6 18.0 %conditional.1 = (f32[4,32,1440]{2,1,0:T(8,128)S(1)}) conditional(s32[]{:T(128)} %convert_element_type.42, f32[4,32,1440]{2,1,0:T(8,128)S(1)} %fusion.22, (f32[4,32,1440]{2,1,0:T(8,128)S(1)}, f32[1440,1536]{1,0:T(8,128)}, pred[4]{0:T(512)(128)(4,1)S(1)}, f32[4]{0:T(128)S(1)}, f32[1,768]{1,0:T(1,128)S(1)}, /*index=5*/s32[768]{0:T(1024)S(1)}) %tuple.45), branch_computations={%region_7.8_spmd, %region_8.9_spmd} | conditional | flops 6795468800 | bytes 25258016 | solution.py:82
  95.9 0.1 fusion.2
  96.0 7.6 %convolution_multiply_fusion = f32[128,1536]{1,0:T(8,128)S(1)} fusion(f32[128,1440]{1,0:T(8,128)S(1)} %bitcast.24, f32[1440,1536]{1,0:T(8,128)} %get-tuple-element.105, f32[128,768]{1,0:T(8,128)S(1)} %bitcast_multiply_fusion), kind=kOutput, calls=%fused_computation.1 | convolution fusion | flops 3397779456 | bytes 10764288 | tf_op jit(solution)/shard_map/cond/branch_1_fun/dot_general | solution.py:57
  103.6 0.3 copy.27
  103.9 9.5 %convolution_subtract_fusion = f32[128,1440]{0,1:T(8,128)S(1)} fusion(f32[128,1440]{0,1:T(8,128)S(1)} %copy.27, f32[128,1536]{1,0:T(8,128)S(1)} %convolution_multiply_fusion, f32[1440,1536]{1,0:T(8,128)} %get-tuple-element.105), kind=kOutput, calls=%fused_computation | convolution fusion | flops 3397570560 | bytes 11108352 | tf_op jit(solution)/shard_map/cond/branch_1_fun/dot_general | solution.py:61
  113.4 0.3 copy.28
  113.6 0.0 copy-start.1
  113.7 0.9 copy-done.1
  (10 shorter events, 0.2 us)
Async XLA Ops:
  0.0 28.8 %copy-start = (f32[4,32,1440]{2,1,0:T(8,128)S(1)}, f32[4,32,1440]{2,1,0:T(8,128)}, u32[]{:S(2)}) copy-start(f32[4,32,1440]{2,1,0:T(8,128)} %param.9) | copy-start | bytes 2211844
  0.0 29.2 %copy-start.2 = (f32[4,32,1440]{2,1,0:T(8,128)S(1)}, f32[4,32,1440]{2,1,0:T(8,128)}, u32[]{:S(2)}) copy-start(f32[4,32,1440]{2,1,0:T(8,128)} %param.10) | copy-start | bytes 2211844
  2.5 89.9 %collective-permute-start = (f32[2,2,32,1440]{3,2,1,0:T(8,128)}, f32[2,2,32,1440]{3,2,1,0:T(8,128)}, u32[]{:S(2)}, u32[]{:S(2)}) collective-permute-start(f32[2,2,32,1440]{3,2,1,0:T(8,128)} %get-tuple-element.115), channel_id=1, source_target_pairs={{0,1},{1,2},{2,3},{3,4},{4,5},{5,6},{6,7},{7,8},{8,9},{9,10},{10,1... | collective-permute-start | bytes 2211848 | tf_op jit(solution)/shard_map/ppermute | solution.py:19
  8.2 84.2 %collective-permute-start.1 = (f32[2,2,32,1440]{3,2,1,0:T(8,128)S(1)}, f32[2,2,32,1440]{3,2,1,0:T(8,128)}, u32[]{:S(2)}, u32[]{:S(2)}) collective-permute-start(f32[2,2,32,1440]{3,2,1,0:T(8,128)S(1)} %get-tuple-element.116), channel_id=1, source_target_pairs={{1,0},{2,1},{3,2},{4,3},{5,4},{6,5},{7,6},{8,7},{9,8},{10,9},{11,1... | collective-permute-start | bytes 2211848 | tf_op jit(solution)/shard_map/ppermute | solution.py:21
  30.2 19.5 %copy-start.5 = (f32[32]{0:T(128)S(1)}, f32[32]{0:T(128)}, u32[]{:S(2)}) copy-start(f32[32]{0:T(128)} %param.12) | copy-start | bytes 388
  30.2 19.6 %slice-start = ((f32[4,32,1440]{2,1,0:T(8,128)}), f32[4,32,1]{2,1,0:T(8,128)S(1)}, s32[]{:S(2)}) async-start(f32[4,32,1440]{2,1,0:T(8,128)} %param.10), calls=%async_computation | async-start | bytes 131072 | tf_op jit(solution)/shard_map/jit(_roll_static)/slice | solution.py:117
  30.2 19.6 %copy-start.4 = (f32[32]{0:T(128)S(1)}, f32[32]{0:T(128)}, u32[]{:S(2)}) copy-start(f32[32]{0:T(128)} %param.13) | copy-start | bytes 388
  84.2 8.2 %copy-start.3 = (f32[4,32,1440]{2,1,0:T(8,128)S(1)}, f32[4,32,1440]{2,1,0:T(8,128)}, u32[]{:S(2)}) copy-start(f32[4,32,1440]{2,1,0:T(8,128)} %param.11) | copy-start | bytes 2211844
  113.6 0.9 copy-start.1
where the time goes:
time: 115 us
  other arithmetic  37.4 us (33%)
  blocking collectives  30 us (26%)
  starting transfers between devices  24.5 us (21%)
  matrix products  17.1 us (15%)
  local copies, waits for them, and re-layouts  3.78 us (3%)
  between operations  1.42 us (1%)
    psum x3, blocking collectives, one_axis_at_a_time(): array = lax.psum(array, axis)  30 us
    sin x1, other arithmetic, transform_table(): return jnp.concatenate([jnp.cos(angle), jnp.sin(angle)], axis=1)  19.5 us
    ppermute x1, starting transfers between devices, padded_2(): lax.ppermute(head, axis, [((i + 1) % count, i) for i in range(ends)])  18.8 us
    dot_general x1, matrix products, filter_units(): lax.dot_general(scaled, table, dims, precision=highest, preferred_element...  9.48 us
    concatenate x1, other arithmetic, transform_table(): return jnp.concatenate([jnp.cos(angle), jnp.sin(angle)], axis=1)  8.16 us
    dot_general x1, matrix products, filter_units(): jnp.dot(flat, table, precision=highest, preferred_element_type=jnp.float32)  7.63 us
    ppermute x1, starting transfers between devices, padded_2(): lax.ppermute(tail, axis, [(i, (i + 1) % count) for i in range(ends)])  5.73 us
    another operation x1, other arithmetic, local(): padded = padded_2(jnp.stack([height, merid_courant]), ((LAT, 1),), 2)  2.49 us
  transfers between devices with their start and end apart: 2, of which 0 were waited for; matrix products, arithmetic and copies ran while one was open for 30% of the time, Pallas kernels for 0%

commit v1 on v0

--- a/solution.py
+++ b/solution.py
@@ -27,7 +27,13 @@
 
 def one_axis_at_a_time(array, axes):
     for axis in axes:
-        array = lax.psum(array, axis)
+
+        def targets_define(vals, along_axis):
+            oldest = lax.all_gather(vals, along_axis)
+            s_next = jnp.sum(oldest, 0)
+            return s_next
+
+        array = targets_define(array, along_axis=axis)
     return array
 
 

time: 115 us -> 124 us (1.078)
  local copies, waits for them, and re-layouts: 3.78 us -> 8.89 us
  between operations: 1.42 us -> 3.59 us
  other arithmetic: 37.4 us -> 39.4 us
    psum x3 -> x0, blocking collectives: 30 us -> none  [one_axis_at_a_time(): array = lax.psum(array, axis)]
    unnamed x0 -> x3, blocking collectives: none -> 29.9 us
    unnamed x12 -> x29, local copies, waits for them, and re-layouts: 0.9 us -> 3.65 us
    reduce_sum x2, other arithmetic: 1 us -> 2.59 us  [local(): partial_sums = jnp.sum(jnp.sum(source, axis=2) * cos_rows[:, None], axis=0)]
  transfers between devices with their start and end apart: 2 -> 2, of which waited for: 0 -> 0; matrix products, arithmetic and copies ran while one was open for 30% -> 33% of each run, Pallas kernels for 0% -> 0%
where the time goes in v1:
time: 124 us
  other arithmetic  39.4 us (32%)
  blocking collectives  29.9 us (24%)
  starting transfers between devices  24.5 us (20%)
  matrix products  17.1 us (14%)
  local copies, waits for them, and re-layouts  8.89 us (7%)
  between operations  3.59 us (3%)
    unnamed x3, blocking collectives  29.9 us
    sin x1, other arithmetic, transform_table(): return jnp.concatenate([jnp.cos(angle), jnp.sin(angle)], axis=1)  19.5 us
    ppermute x1, starting transfers between devices, padded_2(): lax.ppermute(head, axis, [((i + 1) % count, i) for i in range(ends)])  18.8 us
    dot_general x1, matrix products, filter_units(): lax.dot_general(scaled, table, dims, precision=highest, preferred_element...  9.48 us
    concatenate x1, other arithmetic, transform_table(): return jnp.concatenate([jnp.cos(angle), jnp.sin(angle)], axis=1)  8.16 us
    dot_general x1, matrix products, filter_units(): jnp.dot(flat, table, precision=highest, preferred_element_type=jnp.float32)  7.63 us
    ppermute x1, starting transfers between devices, padded_2(): lax.ppermute(tail, axis, [(i, (i + 1) % count) for i in range(ends)])  5.73 us
    unnamed x29, local copies, waits for them, and re-layouts  3.65 us
  transfers between devices with their start and end apart: 2, of which 0 were waited for; matrix products, arithmetic and copies ran while one was open for 33% of the time, Pallas kernels for 0%

profile of v1, /device:TPU:513, one launch (start us, length us, event | category | flops | bytes accessed | tf_op | source)
XLA Modules:
  0.0 123.6 jit_solution(6235333459923784840)
XLA Ops:
  0.0 2.7 %fusion.17 = (f32[2,2,32,1440]{3,2,1,0:T(8,128)}, f32[2,2,32,1440]{3,2,1,0:T(8,128)}) fusion(f32[1,4,32,1440]{3,2,1,0:T(8,128)} %bitcast.24, f32[1,4,32,1440]{3,2,1,0:T(8,128)} %bitcast.30), kind=kLoop, calls=%fused_computation.33 | loop fusion | flops 368640 | bytes 2949120 | tf_op jit(solution)/shard_map/stack | solution.py:118
  2.8 5.7 %collective-permute-start = (f32[2,2,32,1440]{3,2,1,0:T(8,128)}, f32[2,2,32,1440]{3,2,1,0:T(8,128)}, u32[]{:S(2)}, u32[]{:S(2)}) collective-permute-start(f32[2,2,32,1440]{3,2,1,0:T(8,128)} %get-tuple-element.115), channel_id=1, source_target_pairs={{0,1},{1,2},{2,3},{3,4},{4,5},{5,6},{6,7},{7,8},{8,9},{9,10},{10,1... | collective-permute-start | bytes 2211848 | tf_op jit(solution)/shard_map/ppermute | solution.py:19
  8.5 18.8 %collective-permute-start.1 = (f32[2,2,32,1440]{3,2,1,0:T(8,128)}, f32[2,2,32,1440]{3,2,1,0:T(8,128)}, u32[]{:S(2)}, u32[]{:S(2)}) collective-permute-start(f32[2,2,32,1440]{3,2,1,0:T(8,128)} %get-tuple-element.116), channel_id=1, source_target_pairs={{1,0},{2,1},{3,2},{4,3},{5,4},{6,5},{7,6},{8,7},{9,8},{10,9},{11,1... | collective-permute-start | bytes 2211848 | tf_op jit(solution)/shard_map/ppermute | solution.py:21
  27.3 2.9 %fusion.33 = (f32[4,32,1439]{2,1,0:T(8,128)}, f32[4,32,1439]{2,1,0:T(8,128)}) fusion(f32[4,32,1440]{2,1,0:T(8,128)} %param.9), kind=kLoop, calls=%fused_computation.63 | loop fusion | bytes 2947072 | tf_op jit(solution)/shard_map/jit(_roll_static)/slice | solution.py:120
  30.2 0.1 fusion.32
  30.2 0.3 slice.95
  30.5 0.0 copy-done.2
  30.5 1.2 slice.89
  31.7 0.6 sine_reduce_fusion
  32.4 0.0 copy-start.6
  32.4 0.0 copy-start.3
  32.5 0.0 slice-start
  32.5 0.0 copy-start.5
  32.5 19.5 %fusion.7 = (f32[1440,768]{1,0:T(8,128)}, f32[1440,768]{1,0:T(8,128)}) fusion(), kind=kLoop, calls=%fused_computation.15 | loop fusion | flops 9953280 | bytes 8847360 | tf_op jit(solution)/shard_map/sin | solution.py:45
  52.0 0.0 copy-start.7
  52.1 2.5 %fusion.29 = (f32[4,32]{1,0:T(4,128)S(1)}, f32[4,32,1440]{2,1,0:T(8,128)S(1)}) fusion(f32[4,32,1440]{2,1,0:T(8,128)S(1)} %copy-done, f32[32]{0:T(128)S(1)} %copy-done.5, f32[32]{0:T(128)S(1)} %neg.8, f32[4,32,2]{2,1,0:T(8,128)S(1)} %slice.96, f32[4,32,1438]{2,1,0:T(8,128)S(1)} %slice.95, f32[4,32,1439]{2,1,0:T(8,128)} %get-tuple-element.121, ...), kind=kLoop, calls=%fused_computation.51 | loop fusion | flops 3870592 | bytes 5161728 | tf_op jit(solution)/shard_map/reduce_sum | solution.py:127
  54.6 0.1 multiply_reduce_fusion
  54.7 0.7 dynamic-slice
  56.1 0.2 dynamic-update-slice
  56.3 10.7 %all-reduce = f32[256]{0:T(256)S(1)} all-reduce(f32[256]{0:T(256)S(1)} %dynamic-update-slice), channel_id=2, replica_groups=mesh['member'=2,'lat_0'=8,'lat_1'=8,'lat_2'=2] {'lat_0'}, use_global_device_ids=true, to_apply=%add | all-reduce | flops 256 | bytes 2048
  67.0 0.1 reshape.117
  67.1 0.7 dynamic-slice.1
  68.5 0.2 dynamic-update-slice.1
  68.7 10.7 %all-reduce.1 = f32[256]{0:T(256)S(1)} all-reduce(f32[256]{0:T(256)S(1)} %dynamic-update-slice.1), channel_id=3, replica_groups=mesh['member'=2,'lat_0'=8,'lat_1'=8,'lat_2'=2] {'lat_1'}, use_global_device_ids=true, to_apply=%add.1 | all-reduce | flops 256 | bytes 2048
  79.5 0.1 reshape.118
  79.5 0.0 copy-done.7
  79.5 0.7 dynamic-slice.2
  80.9 0.2 dynamic-update-slice.2
  81.2 8.5 %all-reduce.2 = f32[64]{0:T(128)S(1)} all-reduce(f32[64]{0:T(128)S(1)} %dynamic-update-slice.2), channel_id=4, replica_groups=mesh['member'=2,'lat_0'=8,'lat_1'=8,'lat_2'=2] {'lat_2'}, use_global_device_ids=true, to_apply=%add.2 | all-reduce | flops 64 | bytes 512
  89.6 0.1 reshape.119
  89.7 0.1 slice.109
  89.8 1.5 %fusion.31 = (pred[]{:T(512)}, pred[4]{0:T(512)(128)(4,1)S(1)}) fusion(s32[512]{0:T(512)} %param.14, s32[]{:T(128)S(6)} %select_n.50), kind=kLoop, calls=%fused_computation.61 | loop fusion | flops 7 | bytes 25 | tf_op jit(solution)/shard_map/reduce_or | solution.py:88
  91.3 0.8 dynamic-slice_convert_fusion
  93.3 0.0 copy-start.4
  93.3 8.2 %pad_maximum_fusion = f32[1440,1536]{1,0:T(8,128)} fusion(f32[1440,768]{1,0:T(8,128)} %get-tuple-element.123, f32[1440,768]{1,0:T(8,128)} %get-tuple-element.124), kind=kLoop, calls=%fused_computation.8 | loop fusion | flops 2211840 | bytes 17694720 | tf_op jit(solution)/shard_map/concatenate | solution.py:45
  101.5 0.0 collective-permute-done
  101.5 0.0 collective-permute-done.1
  101.5 1.9 %maximum_maximum_fusion = (f32[2,6,32,1440]{3,2,1,0:T(8,128)S(1)}, f32[2,6,32,1440]{3,2,1,0:T(8,128)S(1)}) fusion(f32[1,4,32,1440]{3,2,1,0:T(8,128)S(1)} %bitcast.31, f32[1,4,32,1440]{3,2,1,0:T(8,128)S(1)} %bitcast.25, f32[2,2,32,1440]{3,2,1,0:T(8,128)} %collective-permute-done, f32[2,2,32,1440]{3,2,1,0:T(8,128)} %collective-permute-done.1), kind=kLoop, calls=%fused_computation.18 | loop fusion | flops 2211840 | bytes 7372800 | tf_op jit(solution)/shard_map/concatenate | solution.py:17
  103.5 0.5 fusion.13
  104.0 0.7 fusion.22
  104.7 18.0 %conditional.1 = (f32[4,32,1440]{2,1,0:T(8,128)S(1)}) conditional(s32[]{:T(128)} %convert_element_type.42, f32[4,32,1440]{2,1,0:T(8,128)S(1)} %fusion.22, (f32[4,32,1440]{2,1,0:T(8,128)S(1)}, f32[1440,1536]{1,0:T(8,128)}, pred[4]{0:T(512)(128)(4,1)S(1)}, f32[4]{0:T(128)S(1)}, f32[1,768]{1,0:T(1,128)S(1)}, /*index=5*/s32[768]{0:T(1024)S(1)}) %tuple.45), branch_computations={%region_7.8_spmd, %region_8.9_spmd} | conditional | flops 6795468800 | bytes 25258016 | solution.py:88
  104.9 0.1 fusion.2
  105.1 7.6 %convolution_multiply_fusion = f32[128,1536]{1,0:T(8,128)S(1)} fusion(f32[128,1440]{1,0:T(8,128)S(1)} %bitcast.27, f32[1440,1536]{1,0:T(8,128)} %get-tuple-element.105, f32[128,768]{1,0:T(8,128)S(1)} %bitcast_multiply_fusion), kind=kOutput, calls=%fused_computation.1 | convolution fusion | flops 3397779456 | bytes 10764288 | tf_op jit(solution)/shard_map/cond/branch_1_fun/dot_general | solution.py:63
  112.7 0.3 copy.27
  113.0 9.5 %convolution_subtract_fusion = f32[128,1440]{0,1:T(8,128)S(1)} fusion(f32[128,1440]{0,1:T(8,128)S(1)} %copy.27, f32[128,1536]{1,0:T(8,128)S(1)} %convolution_multiply_fusion, f32[1440,1536]{1,0:T(8,128)} %get-tuple-element.105), kind=kOutput, calls=%fused_computation | convolution fusion | flops 3397570560 | bytes 11108352 | tf_op jit(solution)/shard_map/cond/branch_1_fun/dot_general | solution.py:67
  122.5 0.3 copy.28
  122.7 0.0 copy-start.1
  122.7 0.9 copy-done.1
  (28 shorter events, 0.3 us)
Async XLA Ops:
  0.0 30.2 %copy-start = (f32[4,32,1440]{2,1,0:T(8,128)S(1)}, f32[4,32,1440]{2,1,0:T(8,128)}, u32[]{:S(2)}) copy-start(f32[4,32,1440]{2,1,0:T(8,128)} %param.9) | copy-start | bytes 2211844
  0.0 30.5 %copy-start.2 = (f32[4,32,1440]{2,1,0:T(8,128)S(1)}, f32[4,32,1440]{2,1,0:T(8,128)}, u32[]{:S(2)}) copy-start(f32[4,32,1440]{2,1,0:T(8,128)} %param.10) | copy-start | bytes 2211844
  2.8 98.7 %collective-permute-start = (f32[2,2,32,1440]{3,2,1,0:T(8,128)}, f32[2,2,32,1440]{3,2,1,0:T(8,128)}, u32[]{:S(2)}, u32[]{:S(2)}) collective-permute-start(f32[2,2,32,1440]{3,2,1,0:T(8,128)} %get-tuple-element.115), channel_id=1, source_target_pairs={{0,1},{1,2},{2,3},{3,4},{4,5},{5,6},{6,7},{7,8},{8,9},{9,10},{10,1... | collective-permute-start | bytes 2211848 | tf_op jit(solution)/shard_map/ppermute | solution.py:19
  8.5 93.0 %collective-permute-start.1 = (f32[2,2,32,1440]{3,2,1,0:T(8,128)}, f32[2,2,32,1440]{3,2,1,0:T(8,128)}, u32[]{:S(2)}, u32[]{:S(2)}) collective-permute-start(f32[2,2,32,1440]{3,2,1,0:T(8,128)} %get-tuple-element.116), channel_id=1, source_target_pairs={{1,0},{2,1},{3,2},{4,3},{5,4},{6,5},{7,6},{8,7},{9,8},{10,9},{11,1... | collective-permute-start | bytes 2211848 | tf_op jit(solution)/shard_map/ppermute | solution.py:21
  32.4 19.6 %copy-start.6 = (f32[32]{0:T(128)S(1)}, f32[32]{0:T(128)}, u32[]{:S(2)}) copy-start(f32[32]{0:T(128)} %param.12) | copy-start | bytes 388
  32.4 19.6 %copy-start.3 = (f32[4,32,1440]{2,1,0:T(8,128)S(1)}, f32[4,32,1440]{2,1,0:T(8,128)}, u32[]{:S(2)}) copy-start(f32[4,32,1440]{2,1,0:T(8,128)} %param.10) | copy-start | bytes 2211844
  32.5 19.6 %slice-start = ((f32[4,32,1440]{2,1,0:T(8,128)}), f32[4,32,1]{2,1,0:T(8,128)S(1)}, s32[]{:S(2)}) async-start(f32[4,32,1440]{2,1,0:T(8,128)} %param.10), calls=%async_computation | async-start | bytes 131072 | tf_op jit(solution)/shard_map/jit(_roll_static)/slice | solution.py:123
  32.5 19.6 %copy-start.5 = (f32[32]{0:T(128)S(1)}, f32[32]{0:T(128)}, u32[]{:S(2)}) copy-start(f32[32]{0:T(128)} %param.13) | copy-start | bytes 388
  52.0 2.7 %copy-start.9 = (u32[256]{0:T(256)S(1)}, u32[256]{0:T(256)}, u32[]{:S(2)}) copy-start(u32[256]{0:T(256)} %constant.107) | copy-start | bytes 3076
  52.0 15.1 %copy-start.8 = (u32[256]{0:T(256)S(1)}, u32[256]{0:T(256)}, u32[]{:S(2)}) copy-start(u32[256]{0:T(256)} %constant.112) | copy-start | bytes 3076
  52.0 27.5 %copy-start.7 = (u32[256]{0:T(256)S(1)}, u32[256]{0:T(256)}, u32[]{:S(2)}) copy-start(u32[256]{0:T(256)} %constant.117) | copy-start | bytes 3076
  93.3 8.2 %copy-start.4 = (f32[4,32,1440]{2,1,0:T(8,128)S(1)}, f32[4,32,1440]{2,1,0:T(8,128)}, u32[]{:S(2)}) copy-start(f32[4,32,1440]{2,1,0:T(8,128)} %param.11) | copy-start | bytes 2211844
  122.7 0.9 copy-start.1
